TPU v7x, 32 devices: a whole 2x2x4 slice. The times are simulated.
32 devices in a mesh: member: 2 (over y), lat: 16 (over z, x, core).
Axes of the slice: x: 2, y: 2, z: 4, core: 2. Of those that a mesh axis runs over, the one named last changes fastest.
Arguments:
- tracers: float32 [60, 4, 64, 1440], P('member', None, 'lat'), parts along dimension 0, may hold values from -6 to 6
- currents: float32 [4, 4, 64, 1440], P('member', None, 'lat'), parts along dimension 0, may hold values from -0.4 to 0.4
- column_levels: int32 [128, 1440], P(('member', 'lat')), parts along dimension 0, may hold values from 0 to 4
Outputs:
- advected: float32 [60, 4, 64, 1440], P('member', None, 'lat'), parts along dimension 0
There are 2 independent parts, one for each index of `member`. A program takes and returns all parts, laid end to end along the dimension named above; each array names one. Nothing has to cross between parts.
All inputs are finite; a program needn't handle non-finite values.
Results may differ from a plain program's by a relative error of at most 0.00002.
Values sent between devices are 32-bit elements; how exact they have to be, the bound alone decides.
A program may use at most 64 MiB of HBM per device.

v0:
```python
import functools

import jax
import jax.numpy as jnp
from jax import lax
from jax.experimental import pallas as pl
from jax.experimental.pallas import tpu as pltpu
from jax.sharding import PartitionSpec as P

LANES = 128
WRAP = 4
MESH = pl.DeviceIdType.MESH


def wrapped(x, nlon):
    rest = nlon % LANES
    whole = nlon - rest
    tail = jnp.concatenate([x[:, whole:], x[:, : LANES - rest]], axis=1)
    lane = lax.broadcasted_iota(jnp.int32, tail.shape, 1)
    tail = jnp.where(lane >= LANES - WRAP, pltpu.roll(tail, LANES - rest, 1), tail)
    return jnp.concatenate([x[:, :whole], tail], axis=1)


def face_terms(c, opened):
    c = c * opened * (1.0 / 12.0)
    m = jnp.abs(c)
    return -c - m, 7.0 * c + 3.0 * m, 7.0 * c - 3.0 * m, m - c


def mirrored(tiles, nlon):
    count = len(tiles)
    rest = nlon % LANES
    row = lax.broadcasted_iota(jnp.int32, (LANES, LANES), 0)
    col = lax.broadcasted_iota(jnp.int32, (LANES, LANES), 1)
    near = jnp.where((row + col == rest - 1), 1.0, 0.0).astype(jnp.float32)
    far = jnp.where((row + col == LANES + rest - 1), 1.0, 0.0).astype(jnp.float32)
    dot = functools.partial(
        jnp.dot, precision=lax.Precision.HIGHEST, preferred_element_type=jnp.float32
    )
    return [
        dot(tiles[(count - 1 - q) % count], near) + dot(tiles[(count - 2 - q) % count], far)
        for q in range(count)
    ]


def kernel(
    nlon, levels, start_ref, flow_ref, lev_ref, out_ref,
    lo, hi, flow_lo, flow_hi, lev_lo, lev_hi, coef, wets, field, first,
    send_up, recv_up, send_dn, recv_dn, fsend, frecv,
):
    lat = lax.axis_size("lat")
    me = lax.axis_index("lat")
    width = coef.shape[-1]
    spans = [(q * LANES, min(LANES, nlon - q * LANES)) for q in range(width // LANES)]
    rows = start_ref.shape[0]
    chunks = start_ref.shape[1] // 8
    has_lo = me > 0
    has_hi = me < lat - 1

    barrier = pltpu.get_barrier_semaphore()

    @pl.when(has_lo)
    def _():
        pl.semaphore_signal(barrier, inc=1, device_id={"lat": me - 1}, device_id_type=MESH)

    @pl.when(has_hi)
    def _():
        pl.semaphore_signal(barrier, inc=1, device_id={"lat": me + 1}, device_id_type=MESH)

    @pl.when(has_lo & has_hi)
    def _():
        pl.semaphore_wait(barrier, 2)

    @pl.when(jnp.logical_not(has_lo & has_hi))
    def _():
        pl.semaphore_wait(barrier, 1)

    def remote(src, dst, s, r, target):
        return pltpu.make_async_remote_copy(
            src_ref=src, dst_ref=dst, send_sem=s, recv_sem=r,
            device_id={"lat": target}, device_id_type=MESH,
        )

    def flows(up):
        far = me + 1 if up else me - 1
        base = 0 if up else 3
        n = rows - 1
        part = pl.ds(1, n) if up else pl.ds(0, n)
        dst_f, dst_l = (flow_lo, lev_lo) if up else (flow_hi, lev_hi)
        two = pl.ds(rows - 2, 2) if up else pl.ds(0, 2)
        return [
            remote(lev_ref, dst_l, fsend.at[base], frecv.at[base], far),
            remote(flow_ref.at[1, part], dst_f.at[1, part], fsend.at[base + 1], frecv.at[base + 1], far),
            remote(flow_ref.at[0, two], dst_f.at[0, two], fsend.at[base + 2], frecv.at[base + 2], far),
        ]

    def chunk(up, g):
        part = pl.ds(pl.multiple_of(g * 8, 8), 8)
        if up:
            return remote(start_ref.at[:, part], lo.at[:, part], send_up.at[g], recv_up.at[g], me + 1)
        return remote(start_ref.at[:, part], hi.at[:, part], send_dn.at[g], recv_dn.at[g], me - 1)

    @pl.when(has_hi)
    def _():
        for c in flows(True):
            c.start()

    @pl.when(has_lo)
    def _():
        for c in flows(False):
            c.start()

    def begin(g, carry):
        @pl.when(has_hi)
        def _():
            chunk(True, g).start()

        @pl.when(has_lo)
        def _():
            chunk(False, g).start()

        return carry

    lax.fori_loop(0, chunks, begin, 0)

    @pl.when(jnp.logical_not(has_lo))
    def _():
        flow_lo[...] = jnp.zeros_like(flow_lo)
        lev_lo[...] = jnp.zeros_like(lev_lo)
        lo[...] = jnp.zeros_like(lo)

    def tiles_of(x):
        x = jnp.concatenate([x, jnp.zeros((x.shape[0], width - nlon), x.dtype)], axis=1)
        return [x[:, q * LANES : (q + 1) * LANES] for q in range(width // LANES)]

    @pl.when(jnp.logical_not(has_hi))
    def _():
        for k in range(rows):
            src = rows - 1 - k
            piece = jnp.concatenate([flow_ref[0, src], flow_ref[1, src]], axis=0)
            for (at, n), t in zip(spans, mirrored(tiles_of(piece), nlon)):
                flow_hi[0, k, :, at : at + n] = -t[:levels, :n]
                flow_hi[1, k, :, at : at + n] = -t[levels:, :n]
            lev = jnp.broadcast_to(lev_ref[src : src + 1, :].astype(jnp.float32), (8, nlon))
            for (at, n), t in zip(spans, mirrored(tiles_of(lev), nlon)):
                lev_hi[k : k + 1, at : at + n] = (t[:1, :n] + 0.5).astype(jnp.int32)

        def fold(g, carry):
            part = pl.ds(pl.multiple_of(g * 8, 8), 8)
            x = jnp.concatenate([start_ref[rows - 1 - k, part, :] for k in range(rows)], axis=0)
            for (at, n), t in zip(spans, mirrored(tiles_of(x), nlon)):
                for k in range(rows):
                    hi[k, part, at : at + n] = t[8 * k : 8 * k + 8, :n]
            return carry

        lax.fori_loop(0, chunks, fold, 0)

    @pl.when(has_lo)
    def _():
        for c in flows(True):
            c.wait_recv()

    @pl.when(has_hi)
    def _():
        for c in flows(False):
            c.wait_recv()

    def pick(low, own, high, j):
        if j < 0:
            return low, j + rows
        if j < rows:
            return own, j
        return high, j - rows

    def shift(x, by):
        return pltpu.roll(x, (-by) % width, 1)

    ranks = lax.rem(lax.broadcasted_iota(jnp.int32, (8, nlon), 0), levels)

    for k in range(3 * rows):
        ref, at = pick(lev_lo, lev_ref, lev_hi, k - rows)
        lev = jnp.broadcast_to(ref[at : at + 1, :], (8, nlon))
        wets[k] = wrapped(jnp.where(ranks < lev, 1.0, 0.0), nlon)

    def wet_row(j):
        return wets[j + rows]

    def flow_row(which, j):
        ref, k = pick(flow_lo, flow_ref, flow_hi, j)
        return wrapped(jnp.concatenate([ref[which, k]] * (8 // levels), axis=0), nlon)

    def north_face(j):
        return face_terms(
            0.5 * (flow_row(1, j) + flow_row(1, j + 1)), wet_row(j) * wet_row(j + 1)
        )

    below = north_face(-3)
    for k in range(rows + 4):
        j = k - 2
        wet = wet_row(j)
        u = flow_row(0, j)
        ea, eb, ed, ee = face_terms(0.5 * (u + shift(u, 1)), wet * shift(wet, 1))
        above = north_face(j)
        coef[k, 0] = shift(ea, -1)
        coef[k, 1] = shift(eb, -1) - ea
        coef[k, 2] = shift(ee, -1) - ed
        coef[k, 3] = -ee
        coef[k, 4] = below[0]
        coef[k, 5] = below[1] - above[0]
        coef[k, 6] = below[3] - above[2]
        coef[k, 7] = -above[3]
        coef[k, 8] = 1.0 - eb + shift(ed, -1) - above[1] + below[2]
        below = above

    def section(get, k):
        f = get(0)
        total = coef[k, 8] * f
        total += coef[k, 0] * shift(f, -2)
        total += coef[k, 1] * shift(f, -1)
        total += coef[k, 2] * shift(f, 1)
        total += coef[k, 3] * shift(f, 2)
        total += coef[k, 4] * get(-2)
        total += coef[k, 5] * get(-1)
        total += coef[k, 6] * get(1)
        total += coef[k, 7] * get(2)
        return total

    def step(g, carry):
        @pl.when(has_lo)
        def _():
            chunk(True, g).wait_recv()

        @pl.when(has_hi)
        def _():
            chunk(False, g).wait_recv()

        part = pl.ds(pl.multiple_of(g * 8, 8), 8)

        for k in range(3 * rows):
            ref, at = pick(lo, start_ref, hi, k - rows)
            field[k] = wrapped(ref[at, part, :], nlon) * wets[k]
        for k in range(rows + 4):
            at = k + rows - 2
            first[k] = section(lambda d: field[at + d], k) * wets[at]
        for j in range(rows):
            second = section(lambda d: first[j + 2 + d], j + 2)
            value = 0.5 * (field[j + rows] + second) * wets[j + rows]
            out_ref[part, j, :] = value[:, :nlon]
        return carry

    lax.fori_loop(0, chunks, step, 0)

    @pl.when(has_hi)
    def _():
        for c in flows(True):
            c.wait_send()

    @pl.when(has_lo)
    def _():
        for c in flows(False):
            c.wait_send()

    def finish(g, carry):
        @pl.when(has_hi)
        def _():
            chunk(True, g).wait_send()

        @pl.when(has_lo)
        def _():
            chunk(False, g).wait_send()

        return carry

    lax.fori_loop(0, chunks, finish, 0)


def shards(tracers, currents, column_levels):
    count, levels, rows, nlon = tracers.shape
    width = -(-(nlon + 2 * WRAP) // LANES) * LANES
    start = jnp.transpose(tracers.reshape(count * levels, rows, nlon), (1, 0, 2))
    flow = jnp.transpose(currents, (0, 2, 1, 3))
    chunks = count * levels // 8
    vmem = pl.BlockSpec(memory_space=pltpu.VMEM)
    dma = pltpu.SemaphoreType.DMA
    out = pl.pallas_call(
        functools.partial(kernel, nlon, levels),
        out_shape=jax.ShapeDtypeStruct((count * levels, rows, nlon), jnp.float32),
        in_specs=[vmem] * 3,
        out_specs=vmem,
        scratch_shapes=[
            pltpu.VMEM(start.shape, jnp.float32),
            pltpu.VMEM(start.shape, jnp.float32),
            pltpu.VMEM(flow.shape, jnp.float32),
            pltpu.VMEM(flow.shape, jnp.float32),
            pltpu.VMEM(column_levels.shape, jnp.int32),
            pltpu.VMEM(column_levels.shape, jnp.int32),
            pltpu.VMEM((rows + 4, 9, 8, width), jnp.float32),
            pltpu.VMEM((3 * rows, 8, width), jnp.float32),
            pltpu.VMEM((3 * rows, 8, width), jnp.float32),
            pltpu.VMEM((rows + 4, 8, width), jnp.float32),
            dma((chunks,)), dma((chunks,)), dma((chunks,)), dma((chunks,)),
            dma((6,)), dma((6,)),
        ],
        compiler_params=pltpu.CompilerParams(
            collective_id=0, has_side_effects=True, vmem_limit_bytes=28 * 1024 * 1024
        ),
    )(start, flow, column_levels)
    return out.reshape(tracers.shape)


def solution(mesh):
    in_specs = (
        P("member", None, "lat", None),
        P("member", None, "lat", None),
        P(("member", "lat"), None),
    )
    out_specs = P("member", None, "lat", None)
    return jax.shard_map(shards, mesh=mesh, in_specs=in_specs, out_specs=out_specs, check_vma=False)
```

profile of v0, /device:TPU:9, one launch (start us, length us, event | category | flops | bytes accessed | tf_op | source)
XLA Modules:
  0.0 76.6 jit_solution(14107710627974318378)
XLA Ops:
  0.0 1.0 %copy.10 = f32[2,4,4,1440]{3,1,2,0:T(4,128)S(1)} copy(f32[2,4,4,1440]{3,2,1,0:T(4,128)} %param.4) | data formatting | bytes 368640 | tf_op args[1]
  1.0 0.0 copy-start
  1.0 2.8 %copy.9 = f32[120,4,1440]{2,0,1:T(8,128)S(1)} copy(f32[120,4,1440]{2,1,0:T(4,128)} %bitcast.11) | data formatting | bytes 5529600 | tf_op jit(solution)/shard_map/reshape | solution.py:280
  3.8 0.0 copy-done
  3.8 71.1 %shard_map.37 = f32[120,4,1440]{2,1,0:T(4,128)S(1)} custom-call(f32[4,120,1440]{2,1,0:T(8,128)S(1)} %bitcast.9, f32[2,4,4,1440]{3,2,1,0:T(4,128)S(1)} %bitcast.10, s32[4,1440]{1,0:T(4,128)S(1)} %copy-done), custom_call_target="tpu_custom_call" | custom-call | tf_op jit(solution)/shard_map/pallas_call | solution.py:285
  75.0 1.6 %copy.12 = f32[30,4,4,1440]{3,2,1,0:T(4,128)} copy(f32[30,4,4,1440]{3,2,1,0:T(4,128)S(1)} %bitcast.8) | data formatting | bytes 5529600
Async XLA Ops:
  1.0 2.8 %copy-start = (s32[4,1440]{1,0:T(4,128)S(1)}, s32[4,1440]{1,0:T(4,128)}, u32[]{:S(2)}) copy-start(s32[4,1440]{1,0:T(4,128)} %lev_ref.1) | copy-start | bytes 69124
where the time goes:
time: 76.7 us; the launch traced here: 76.6 us
  Pallas kernels  71.1 us (93%)
  local copies, waits for them, and re-layouts  5.4 us (7%)
    pallas_call x1, Pallas kernels, shards(): pl.pallas_call(functools.partial(kernel, nlon, levels), out_shape=jax.Sha...  71.1 us
    reshape x1, local copies, waits for them, and re-layouts, shards(): tracers.reshape(count * levels, rows, nlon)  2.79 us
    unnamed x4, local copies, waits for them, and re-layouts  2.61 us

commit v1 on v0

--- a/solution.py
+++ b/solution.py
@@ -19,6 +19,15 @@
     lane = lax.broadcasted_iota(jnp.int32, tail.shape, 1)
     tail = jnp.where(lane >= LANES - WRAP, pltpu.roll(tail, LANES - rest, 1), tail)
     return jnp.concatenate([x[:, :whole], tail], axis=1)
+
+
+def joined(main, pack, k, rest):
+    lane = lax.broadcasted_iota(jnp.int32, pack.shape, 1)
+    east = pltpu.roll(pack, (-k * rest) % LANES, 1)
+    west = pltpu.roll(pack, (-(k + 1) * rest) % LANES, 1)
+    tail = jnp.where(lane < rest, east, pltpu.roll(main[:, :LANES], rest, 1))
+    tail = jnp.where(lane >= LANES - WRAP, west, tail)
+    return jnp.concatenate([main, tail], axis=1)
 
 
 def face_terms(c, opened):
@@ -45,7 +54,7 @@
 
 def kernel(
     nlon, levels, start_ref, flow_ref, lev_ref, out_ref,
-    lo, hi, flow_lo, flow_hi, lev_lo, lev_hi, coef, wets, field, first,
+    lo, hi, pack, pack_lo, pack_hi, flow_lo, flow_hi, lev_lo, lev_hi, coef, wets, field, first,
     send_up, recv_up, send_dn, recv_dn, fsend, frecv,
 ):
     lat = lax.axis_size("lat")
@@ -53,6 +62,8 @@
     width = coef.shape[-1]
     spans = [(q * LANES, min(LANES, nlon - q * LANES)) for q in range(width // LANES)]
     rows = start_ref.shape[0]
+    rest = nlon % LANES
+    whole = nlon - rest
     chunks = start_ref.shape[1] // 8
     has_lo = me > 0
     has_hi = me < lat - 1
@@ -66,6 +77,10 @@
     @pl.when(has_hi)
     def _():
         pl.semaphore_signal(barrier, inc=1, device_id={"lat": me + 1}, device_id_type=MESH)
+
+    for g in range(chunks):
+        part = pl.ds(g * 8, 8)
+        pack[part, :] = jnp.concatenate([start_ref[k, part, whole:] for k in range(rows)], axis=1)
 
     @pl.when(has_lo & has_hi)
     def _():
@@ -83,7 +98,8 @@
 
     def flows(up):
         far = me + 1 if up else me - 1
-        base = 0 if up else 3
+        base = 0 if up else 4
+        dst_p = pack_lo if up else pack_hi
         n = rows - 1
         part = pl.ds(1, n) if up else pl.ds(0, n)
         dst_f, dst_l = (flow_lo, lev_lo) if up else (flow_hi, lev_hi)
@@ -92,13 +108,15 @@
             remote(lev_ref, dst_l, fsend.at[base], frecv.at[base], far),
             remote(flow_ref.at[1, part], dst_f.at[1, part], fsend.at[base + 1], frecv.at[base + 1], far),
             remote(flow_ref.at[0, two], dst_f.at[0, two], fsend.at[base + 2], frecv.at[base + 2], far),
+            remote(pack, dst_p, fsend.at[base + 3], frecv.at[base + 3], far),
         ]
 
     def chunk(up, g):
         part = pl.ds(pl.multiple_of(g * 8, 8), 8)
+        main = start_ref.at[:, part, pl.ds(0, whole)]
         if up:
-            return remote(start_ref.at[:, part], lo.at[:, part], send_up.at[g], recv_up.at[g], me + 1)
-        return remote(start_ref.at[:, part], hi.at[:, part], send_dn.at[g], recv_dn.at[g], me - 1)
+            return remote(main, lo.at[:, part], send_up.at[g], recv_up.at[g], me + 1)
+        return remote(main, hi.at[:, part], send_dn.at[g], recv_dn.at[g], me - 1)
 
     @pl.when(has_hi)
     def _():
@@ -128,6 +146,7 @@
         flow_lo[...] = jnp.zeros_like(flow_lo)
         lev_lo[...] = jnp.zeros_like(lev_lo)
         lo[...] = jnp.zeros_like(lo)
+        pack_lo[...] = jnp.zeros_like(pack_lo)
 
     def tiles_of(x):
         x = jnp.concatenate([x, jnp.zeros((x.shape[0], width - nlon), x.dtype)], axis=1)
@@ -148,9 +167,12 @@
         def fold(g, carry):
             part = pl.ds(pl.multiple_of(g * 8, 8), 8)
             x = jnp.concatenate([start_ref[rows - 1 - k, part, :] for k in range(rows)], axis=0)
-            for (at, n), t in zip(spans, mirrored(tiles_of(x), nlon)):
+            tiles = mirrored(tiles_of(x), nlon)
+            for (at, n), t in zip(spans[:-1], tiles[:-1]):
                 for k in range(rows):
                     hi[k, part, at : at + n] = t[8 * k : 8 * k + 8, :n]
+            ends = [tiles[-1][8 * k : 8 * k + 8, :rest] for k in range(rows)]
+            pack_hi[part, :] = jnp.concatenate(ends, axis=1)
             return carry
 
         lax.fori_loop(0, chunks, fold, 0)
@@ -238,7 +260,8 @@
 
         for k in range(3 * rows):
             ref, at = pick(lo, start_ref, hi, k - rows)
-            field[k] = wrapped(ref[at, part, :], nlon) * wets[k]
+            ends, _ = pick(pack_lo, pack, pack_hi, k - rows)
+            field[k] = joined(ref[at, part, :whole], ends[part, :], at, rest) * wets[k]
         for k in range(rows + 4):
             at = k + rows - 2
             first[k] = section(lambda d: field[at + d], k) * wets[at]
@@ -288,8 +311,11 @@
         in_specs=[vmem] * 3,
         out_specs=vmem,
         scratch_shapes=[
-            pltpu.VMEM(start.shape, jnp.float32),
-            pltpu.VMEM(start.shape, jnp.float32),
+            pltpu.VMEM((rows, count * levels, nlon - nlon % LANES), jnp.float32),
+            pltpu.VMEM((rows, count * levels, nlon - nlon % LANES), jnp.float32),
+            pltpu.VMEM((count * levels, LANES), jnp.float32),
+            pltpu.VMEM((count * levels, LANES), jnp.float32),
+            pltpu.VMEM((count * levels, LANES), jnp.float32),
             pltpu.VMEM(flow.shape, jnp.float32),
             pltpu.VMEM(flow.shape, jnp.float32),
             pltpu.VMEM(column_levels.shape, jnp.int32),
@@ -299,7 +325,7 @@
             pltpu.VMEM((3 * rows, 8, width), jnp.float32),
             pltpu.VMEM((rows + 4, 8, width), jnp.float32),
             dma((chunks,)), dma((chunks,)), dma((chunks,)), dma((chunks,)),
-            dma((6,)), dma((6,)),
+            dma((8,)), dma((8,)),
         ],
         compiler_params=pltpu.CompilerParams(
             collective_id=0, has_side_effects=True, vmem_limit_bytes=28 * 1024 * 1024

time: 76.7 us -> 73 us (0.952)
  Pallas kernels: 71.1 us -> 67.4 us
    pallas_call x1, Pallas kernels: 71.1 us -> 67.4 us  [shards(): pl.pallas_call(functools.partial(kernel, nlon, levels), out_shape=jax.Sha...]
where the time goes in v1:
time: 73 us; the launch traced here: 72.8 us
  Pallas kernels  67.4 us (92%)
  local copies, waits for them, and re-layouts  5.4 us (7%)
    pallas_call x1, Pallas kernels, shards(): pl.pallas_call(functools.partial(kernel, nlon, levels), out_shape=jax.Sha...  67.4 us
    reshape x1, local copies, waits for them, and re-layouts, shards(): tracers.reshape(count * levels, rows, nlon)  2.79 us
    unnamed x4, local copies, waits for them, and re-layouts  2.61 us

profile of v1, /device:TPU:9, one launch (start us, length us, event | category | flops | bytes accessed | tf_op | source)
XLA Modules:
  0.0 72.8 jit_solution(1247753046928980340)
XLA Ops:
  0.0 1.0 %copy.10 = f32[2,4,4,1440]{3,1,2,0:T(4,128)S(1)} copy(f32[2,4,4,1440]{3,2,1,0:T(4,128)} %param.4) | data formatting | bytes 368640 | tf_op args[1]
  1.0 0.0 copy-start
  1.0 2.8 %copy.9 = f32[120,4,1440]{2,0,1:T(8,128)S(1)} copy(f32[120,4,1440]{2,1,0:T(4,128)} %bitcast.11) | data formatting | bytes 5529600 | tf_op jit(solution)/shard_map/reshape | solution.py:303
  3.8 0.0 copy-done
  3.8 67.4 %shard_map.37 = f32[120,4,1440]{2,1,0:T(4,128)S(1)} custom-call(f32[4,120,1440]{2,1,0:T(8,128)S(1)} %bitcast.9, f32[2,4,4,1440]{3,2,1,0:T(4,128)S(1)} %bitcast.10, s32[4,1440]{1,0:T(4,128)S(1)} %copy-done), custom_call_target="tpu_custom_call" | custom-call | tf_op jit(solution)/shard_map/pallas_call | solution.py:308
  71.2 1.6 %copy.12 = f32[30,4,4,1440]{3,2,1,0:T(4,128)} copy(f32[30,4,4,1440]{3,2,1,0:T(4,128)S(1)} %bitcast.8) | data formatting | bytes 5529600
Async XLA Ops:
  1.0 2.8 %copy-start = (s32[4,1440]{1,0:T(4,128)S(1)}, s32[4,1440]{1,0:T(4,128)}, u32[]{:S(2)}) copy-start(s32[4,1440]{1,0:T(4,128)} %lev_ref.1) | copy-start | bytes 69124

commit v2 on v1

--- a/solution.py
+++ b/solution.py
@@ -53,8 +53,8 @@
 
 
 def kernel(
-    nlon, levels, start_ref, flow_ref, lev_ref, out_ref,
-    lo, hi, pack, pack_lo, pack_hi, flow_lo, flow_hi, lev_lo, lev_hi, coef, wets, field, first,
+    nlon, levels, raw_ref, raw_flow, lev_ref, out_ref,
+    start_ref, flow_ref, lo, hi, pack, pack_lo, pack_hi, flow_lo, flow_hi, lev_lo, lev_hi, coef, wets, field, first,
     send_up, recv_up, send_dn, recv_dn, fsend, frecv,
 ):
     lat = lax.axis_size("lat")
@@ -80,7 +80,18 @@
 
     for g in range(chunks):
         part = pl.ds(g * 8, 8)
-        pack[part, :] = jnp.concatenate([start_ref[k, part, whole:] for k in range(rows)], axis=1)
+        pack[part, :] = jnp.concatenate([raw_ref[part, k, whole:] for k in range(rows)], axis=1)
+
+    for k in range(rows):
+        for which in range(2):
+            flow_ref[which, k] = raw_flow[which, :, k, :]
+
+    def reorder(g):
+        part = pl.ds(pl.multiple_of(g * 8, 8), 8)
+        for k in range(rows):
+            start_ref[k, part, :] = raw_ref[part, k, :]
+
+    reorder(0)
 
     @pl.when(has_lo & has_hi)
     def _():
@@ -129,6 +140,10 @@
             c.start()
 
     def begin(g, carry):
+        @pl.when(g < chunks - 1)
+        def _():
+            reorder(g + 1)
+
         @pl.when(has_hi)
         def _():
             chunk(True, g).start()
@@ -300,8 +315,7 @@
 def shards(tracers, currents, column_levels):
     count, levels, rows, nlon = tracers.shape
     width = -(-(nlon + 2 * WRAP) // LANES) * LANES
-    start = jnp.transpose(tracers.reshape(count * levels, rows, nlon), (1, 0, 2))
-    flow = jnp.transpose(currents, (0, 2, 1, 3))
+    raw = tracers.reshape(count * levels, rows, nlon)
     chunks = count * levels // 8
     vmem = pl.BlockSpec(memory_space=pltpu.VMEM)
     dma = pltpu.SemaphoreType.DMA
@@ -311,13 +325,15 @@
         in_specs=[vmem] * 3,
         out_specs=vmem,
         scratch_shapes=[
+            pltpu.VMEM((rows, count * levels, nlon), jnp.float32),
+            pltpu.VMEM((2, rows, levels, nlon), jnp.float32),
             pltpu.VMEM((rows, count * levels, nlon - nlon % LANES), jnp.float32),
             pltpu.VMEM((rows, count * levels, nlon - nlon % LANES), jnp.float32),
             pltpu.VMEM((count * levels, LANES), jnp.float32),
             pltpu.VMEM((count * levels, LANES), jnp.float32),
             pltpu.VMEM((count * levels, LANES), jnp.float32),
-            pltpu.VMEM(flow.shape, jnp.float32),
-            pltpu.VMEM(flow.shape, jnp.float32),
+            pltpu.VMEM((2, rows, levels, nlon), jnp.float32),
+            pltpu.VMEM((2, rows, levels, nlon), jnp.float32),
             pltpu.VMEM(column_levels.shape, jnp.int32),
             pltpu.VMEM(column_levels.shape, jnp.int32),
             pltpu.VMEM((rows + 4, 9, 8, width), jnp.float32),
@@ -330,7 +346,7 @@
         compiler_params=pltpu.CompilerParams(
             collective_id=0, has_side_effects=True, vmem_limit_bytes=28 * 1024 * 1024
         ),
-    )(start, flow, column_levels)
+    )(raw, currents, column_levels)
     return out.reshape(tracers.shape)
 
 

time: 73 us -> 72.8 us (level)
    reshape x1 -> x0, local copies, waits for them, and re-layouts: 2.79 us -> none  [shards(): tracers.reshape(count * levels, rows, nlon)]
    unnamed x4 -> x7, local copies, waits for them, and re-layouts: 2.61 us -> 5.1 us
where the time goes in v2:
time: 72.8 us; the launch traced here: 72.5 us
  Pallas kernels  67.4 us (93%)
  local copies, waits for them, and re-layouts  5.1 us (7%)
    pallas_call x1, Pallas kernels, shards(): pl.pallas_call(functools.partial(kernel, nlon, levels), out_shape=jax.Sha...  67.4 us
    unnamed x7, local copies, waits for them, and re-layouts  5.1 us

profile of v2, /device:TPU:9, one launch (start us, length us, event | category | flops | bytes accessed | tf_op | source)
XLA Modules:
  0.0 72.5 jit_solution(2245163574801135832)
XLA Ops:
  0.0 0.0 copy-start
  0.0 1.8 %copy-done = f32[30,4,4,1440]{3,2,1,0:T(4,128)S(1)} copy-done((f32[30,4,4,1440]{3,2,1,0:T(4,128)S(1)}, f32[30,4,4,1440]{3,2,1,0:T(4,128)}, u32[]{:S(2)}) %copy-start) | copy-done | bytes 2764824
  1.8 0.0 copy-start.1
  1.8 0.9 %copy-done.1 = f32[2,4,4,1440]{3,2,1,0:T(4,128)S(1)} copy-done((f32[2,4,4,1440]{3,2,1,0:T(4,128)S(1)}, f32[2,4,4,1440]{3,2,1,0:T(4,128)}, u32[]{:S(2)}) %copy-start.1) | copy-done | bytes 184344
  2.8 0.0 copy-start.2
  2.8 0.7 %copy-done.2 = s32[4,1440]{1,0:T(4,128)S(1)} copy-done((s32[4,1440]{1,0:T(4,128)S(1)}, s32[4,1440]{1,0:T(4,128)}, u32[]{:S(2)}) %copy-start.2) | copy-done | bytes 23064
  3.5 67.4 %shard_map.37 = f32[120,4,1440]{2,1,0:T(4,128)S(1)} custom-call(f32[120,4,1440]{2,1,0:T(4,128)S(1)} %bitcast.3, f32[2,4,4,1440]{3,2,1,0:T(4,128)S(1)} %copy-done.1, s32[4,1440]{1,0:T(4,128)S(1)} %copy-done.2), custom_call_target="tpu_custom_call" | custom-call | tf_op jit(solution)/shard_map/pallas_call | solution.py:322
  70.9 1.6 %copy.5 = f32[30,4,4,1440]{3,2,1,0:T(4,128)} copy(f32[30,4,4,1440]{3,2,1,0:T(4,128)S(1)} %bitcast.2) | data formatting | bytes 5529600
Async XLA Ops:
  0.0 1.8 %copy-start = (f32[30,4,4,1440]{3,2,1,0:T(4,128)S(1)}, f32[30,4,4,1440]{3,2,1,0:T(4,128)}, u32[]{:S(2)}) copy-start(f32[30,4,4,1440]{3,2,1,0:T(4,128)} %param.3) | copy-start | bytes 8294404
  1.8 0.9 %copy-start.1 = (f32[2,4,4,1440]{3,2,1,0:T(4,128)S(1)}, f32[2,4,4,1440]{3,2,1,0:T(4,128)}, u32[]{:S(2)}) copy-start(f32[2,4,4,1440]{3,2,1,0:T(4,128)} %raw_flow.1) | copy-start | bytes 552964
  2.8 0.7 %copy-start.2 = (s32[4,1440]{1,0:T(4,128)S(1)}, s32[4,1440]{1,0:T(4,128)}, u32[]{:S(2)}) copy-start(s32[4,1440]{1,0:T(4,128)} %lev_ref.1) | copy-start | bytes 69124
